TPU v7x, 32 devices: a whole 2x2x4 slice. The times are simulated.
32 devices in a mesh: seq: 4 (over y, x), seg: 4 (over z), head: 2 (over core).
Axes of the slice: x: 2, y: 2, z: 4, core: 2. Of those that a mesh axis runs over, the one named last changes fastest.
Arguments:
- queries: bfloat16 [8, 16384, 128], P('head', ('seg', 'seq')), may hold values from -6 to 6
- keys: bfloat16 [8, 16384, 128], P('head', ('seg', 'seq')), may hold values from -6 to 6
- values: bfloat16 [8, 16384, 128], P('head', ('seg', 'seq')), may hold values from -8 to 8
- teacher: bfloat16 [8, 16384, 128], P('head', ('seg', 'seq')), may hold values from -6 to 6
- query_proj: float32 [128, 16], replicated, may hold values from -0.5 to 0.5
- key_proj: float32 [128, 16], replicated, may hold values from -0.5 to 0.5
Outputs:
- student: bfloat16 [8, 16384, 128], P('head', ('seg', 'seq'))
- query_grad: float32 [128, 16], replicated
- key_grad: float32 [128, 16], replicated
All inputs are finite; a program needn't handle non-finite values.
Results may differ from a plain program's by a relative error of at most 0.0014.
The roundings to bfloat16 on the way count: a program that leaves them out, or rounds other values in their place, can miss the bound.
Values sent between devices are 32-bit elements; how exact they have to be, the bound alone decides.
No kernel may reach another device: no remote copies, remote signals or barrier semaphores. Data moves between devices by JAX's collectives and lax.ppermute only.
A program may use at most 64 MiB of HBM per device.

v0:
```python
import math
import jax
import jax.numpy as jnp
import numpy as np
from jax import lax
from jax.sharding import PartitionSpec as P

highest = lax.Precision.HIGHEST


def carried_in(value, axis, join, neutral, backward):
    count, mine = (lax.axis_size(axis), lax.axis_index(axis))
    pieces = jax.tree.map(lambda part: lax.all_gather(part, axis), value)
    if backward:
        pieces = jax.tree.map(lambda part: part[::-1], pieces)
        mine = count - 1 - mine
    running = jax.tree.map(
        lambda part, zero: jnp.full_like(part, 0) + jnp.asarray(zero, part.dtype), value, neutral
    )

    def step(position, running):
        longer = join(running, jax.tree.map(lambda part: part[position], pieces))
        return jax.tree.map(lambda new, old: jnp.where(position < mine, new, old), longer, running)

    return lax.fori_loop(0, count - 1, step, running)


def feature_tables(width):
    first, second = np.triu_indices(width)
    eye = np.eye(width)
    coef = np.where(first == second, 0.5**0.5, 1.0)
    return (
        jnp.asarray(eye[first], jnp.float32),
        jnp.asarray(eye[second], jnp.float32),
        jnp.asarray(coef, jnp.float32),
    )


def features(proj_t, tables):
    sel_a, sel_b, coef = tables
    left = jnp.dot(sel_a, proj_t, precision=highest)
    right = jnp.dot(sel_b, proj_t, precision=highest)
    return jnp.concatenate([jnp.ones_like(proj_t[:1]), proj_t, coef[:, None] * left * right], 0)


def feature_grad(proj_t, grad_phi, tables):
    sel_a, sel_b, coef = tables
    width = proj_t.shape[0]
    left = jnp.dot(sel_a, proj_t, precision=highest)
    right = jnp.dot(sel_b, proj_t, precision=highest)
    quad = grad_phi[1 + width :] * coef[:, None]
    return (
        grad_phi[1 : 1 + width]
        + jnp.dot(sel_a.T, quad * right, precision=highest)
        + jnp.dot(sel_b.T, quad * left, precision=highest)
    )


def project(weight_b, rows):
    return lax.dot_general(
        weight_b, rows, (((0,), (1,)), ((), ())), preferred_element_type=jnp.float32
    )


def head_state(q_h, k_h, v_h, wq_b, wk_b, tables):
    q_t = project(wq_b, q_h)
    k_t = project(wk_b, k_h)
    phi_k = features(k_t, tables)
    state = jnp.dot(phi_k.astype(jnp.bfloat16), v_h, preferred_element_type=jnp.float32)
    return (q_t, k_t, state, jnp.sum(phi_k, 1))


def head_forward(q_t, k_t, v_h, teacher_h, s_prev, z_prev, scale, tables):
    phi_q = features(q_t, tables)
    length = q_t.shape[1]
    scores = lax.dot_general(q_t, k_t, (((0,), (0,)), ((), ())), precision=highest)
    causal = jnp.arange(length)[:, None] >= jnp.arange(length)[None, :]
    weights = jnp.where(causal, 1.0 + scores + 0.5 * scores * scores, 0.0)
    numer = jnp.dot(weights.astype(jnp.bfloat16), v_h, preferred_element_type=jnp.float32)
    numer = numer + lax.dot_general(phi_q, s_prev, (((0,), (0,)), ((), ())), precision=highest)
    denom = jnp.sum(weights, 1) + jnp.dot(z_prev, phi_q, precision=highest)
    student = numer / denom[:, None]
    g_out = scale * (student - teacher_h.astype(jnp.float32))
    g_numer = g_out / denom[:, None]
    g_denom = -jnp.sum(g_out * student, 1) / denom
    g_weights = (
        lax.dot_general(
            g_numer.astype(jnp.bfloat16),
            v_h,
            (((1,), (1,)), ((), ())),
            preferred_element_type=jnp.float32,
        )
        + g_denom[:, None]
    )
    g_scores = jnp.where(causal, g_weights * (1.0 + scores), 0.0)
    g_q = lax.dot_general(k_t, g_scores, (((1,), (1,)), ((), ())), precision=highest)
    g_k = jnp.dot(q_t, g_scores, precision=highest)
    g_phi_q = (
        lax.dot_general(s_prev, g_numer, (((1,), (1,)), ((), ())), precision=highest)
        + z_prev[:, None] * g_denom[None, :]
    )
    g_q = g_q + feature_grad(q_t, g_phi_q, tables)
    g_state = jnp.dot(phi_q, g_numer, precision=highest)
    h_state = jnp.dot(phi_q, g_denom, precision=highest)
    return (student, g_q, g_k, g_state, h_state)


def head_grads(q_h, k_h, v_h, k_t, g_q, g_k, g_next, h_next, tables):
    g_phi_k = (
        lax.dot_general(
            g_next.astype(jnp.bfloat16),
            v_h,
            (((1,), (1,)), ((), ())),
            preferred_element_type=jnp.float32,
        )
        + h_next[:, None]
    )
    g_k = g_k + feature_grad(k_t, g_phi_k, tables)
    grad_q = lax.dot_general(
        q_h, g_q.astype(jnp.bfloat16), (((0,), (1,)), ((), ())), preferred_element_type=jnp.float32
    )
    grad_k = lax.dot_general(
        k_h, g_k.astype(jnp.bfloat16), (((0,), (1,)), ((), ())), preferred_element_type=jnp.float32
    )
    return (grad_q, grad_k)


def add_trees(first, second):
    return jax.tree.map(jnp.add, first, second)


def masked_fold(mine, backward, carry, piece):
    rows = piece[0].shape[0]
    index = jnp.arange(rows)
    keep = index > mine if backward else index < mine

    def pick(array):
        shaped = keep.reshape((rows,) + (1,) * (array.ndim - 1))
        return jnp.sum(jnp.where(shaped, array, 0.0), 0)

    part = jax.tree.map(pick, piece)
    whole = jax.tree.map(lambda array: jnp.sum(array, 0), piece)
    return (add_trees(carry[0], part), add_trees(carry[1], whole))


def carried(local, backward):
    zeros = jax.tree.map(jnp.zeros_like, local)
    stacked = jax.tree.map(lambda array: array[None], local)
    inner, totals = masked_fold(
        lax.axis_index("seq"),
        backward,
        (zeros, zeros),
        (
            lax.all_gather(stacked[0], "seq", axis=0, tiled=True),
            lax.all_gather(stacked[1], "seq", axis=0, tiled=True),
        ),
    )
    outer = carried_in(totals, "seg", add_trees, zeros, backward)
    return add_trees(inner, outer)


def shards(queries, keys, values, teacher, query_proj, key_proj):
    tables = feature_tables(query_proj.shape[1])
    wq_b = query_proj.astype(jnp.bfloat16)
    wk_b = key_proj.astype(jnp.bfloat16)
    q_t, k_t, states, counts = lax.map(
        lambda xs: head_state(xs[0], xs[1], xs[2], wq_b, wk_b, tables), (queries, keys, values)
    )
    s_prev, z_prev = carried((states, counts), False)
    heads_all = queries.shape[0] * lax.axis_size("head")
    tokens_all = queries.shape[1] * lax.axis_size("seq") * lax.axis_size("seg")
    scale = 1.0 / math.sqrt(heads_all * tokens_all)
    student, g_q, g_k, g_state, h_state = lax.map(
        lambda xs: head_forward(xs[0], xs[1], xs[2], xs[3], xs[4], xs[5], scale, tables),
        (q_t, k_t, values, teacher, s_prev, z_prev),
    )
    g_next, h_next = carried((g_state, h_state), True)
    grad_q, grad_k = lax.map(
        lambda xs: head_grads(xs[0], xs[1], xs[2], xs[3], xs[4], xs[5], xs[6], xs[7], tables),
        (queries, keys, values, k_t, g_q, g_k, g_next, h_next),
    )
    summed = lax.psum((jnp.sum(grad_q, 0), jnp.sum(grad_k, 0)), ("seq", "seg", "head"))
    return (student.astype(jnp.bfloat16), summed[0], summed[1])


def solution(mesh):
    in_specs = (
        P("head", ("seg", "seq"), None),
        P("head", ("seg", "seq"), None),
        P("head", ("seg", "seq"), None),
        P("head", ("seg", "seq"), None),
        P(),
        P(),
    )
    out_specs = (P("head", ("seg", "seq"), None), P(), P())
    return jax.shard_map(shards, mesh=mesh, in_specs=in_specs, out_specs=out_specs, check_vma=False)
```

profile of v0, /device:TPU:0, one launch (start us, length us, event | category | flops | bytes accessed | tf_op | source)
XLA Modules:
  0.0 344.7 jit_solution(8274270570329167139)
XLA Ops:
  8.7 27.1 %while.81 = (s32[]{:T(128)}, f32[4,16,1024]{2,1,0:T(8,128)S(1)}, f32[4,16,1024]{2,1,0:T(8,128)S(1)}, f32[4,153,128]{2,1,0:T(8,128)S(1)}, f32[4,153]{1,0:T(4,128)...) while((s32[]{:T(128)}, f32[4,16,1024]{2,1,0:T(8,128)S(1)}, ...), condition=%wide.region_2.3_spmd.clone, body=%wide.region_0.2_spmd.sunk.clone.sunk | while | flops 103662440 | bytes 4145861 | solution.py:166
  36.6 31.5 %all-gather.17.cloned.1.call-done = f32[16,153,128]{2,1,0:T(8,128)} async-done(((f32[4,153,128]{2,1,0:T(8,128)}), f32[16,153,128]{2,1,0:T(8,128)}) %all-gather.17.cloned.1.call-update) | async-done | bytes 1253392 | tf_op jit(solution)/shard_map/all_gather | solution.py:154
  68.1 2.4 fusion.90
  70.6 8.1 %all-gather.8 = f32[4,4,153]{2,1,0:T(4,128)S(1)} all-gather(f32[1,4,153]{2,1,0:T(4,128)S(1)} %bitcast.304), channel_id=4, replica_groups=mesh['seq'=4,'seg'=4,'head'=2] {'seq'}, dimensions={0}, use_global_device_ids=true | all-gather | bytes 12240 | tf_op jit(solution)/shard_map/all_gather | solution.py:155
  78.8 13.7 %all-gather.9 = f32[4,4,153]{2,1,0:T(4,128)S(1)} all-gather(f32[1,4,153]{2,1,0:T(4,128)S(1)} %bitcast.301), channel_id=5, replica_groups=mesh['seq'=4,'seg'=4,'head'=2] {'seg'}, dimensions={0}, use_global_device_ids=true | all-gather | bytes 12240 | tf_op jit(solution)/shard_map/all_gather | solution.py:13
  93.2 10.2 %all-gather.19.cloned.1.call-done = f32[16,153,128]{2,1,0:T(8,128)} async-done(((f32[4,153,128]{2,1,0:T(8,128)}), f32[16,153,128]{2,1,0:T(8,128)}) %all-gather.19.cloned.1.call-update) | async-done | bytes 1253392 | tf_op jit(solution)/shard_map/all_gather | solution.py:13
  103.4 3.4 while.84
  109.1 98.5 %while.82 = (s32[]{:T(128)}, bf16[4,1024,128]{2,1,0:T(8,128)(2,1)}, bf16[4,16,1024]{2,1,0:T(8,128)(2,1)}, f32[4,16,1024]{2,1,0:T(8,128)}, f32[4,153,128]{2,1,0:T...) while((s32[]{:T(128)}, bf16[4,1024,128]{2,1,0:T(8,128)(2,1)}, ...), condition=%wide.region_12.13_spmd.clone, body=%wide.region_9.12_spmd.sunk.clone.sunk | while | flops 1998507008 | bytes 75882544 | solution.py:173
  110.4 3.8 %fusion.212 = (f32[1024]{0:T(1024)S(1)}, f32[1024,1024]{0,1:T(8,128)S(1)}) fusion(f32[16,1024]{1,0:T(8,128)S(1)} %dynamic-slice_bitcast_fusion.2, f32[4,16,1024]{2,1,0:T(8,128)S(1)} %get-tuple-element.1167, s32[]{:T(128)S(6)} %copy.77), kind=kOutput, calls=%fused_computation.28.clone.1 | convolution fusion | flops 208665600 | bytes 4329476 | tf_op jit(solution)/shard_map/while/body/eval_jaxpr/dot_general | solution.py:76
  127.4 4.2 %fusion.218 = f32[4,16,1024]{2,1,0:T(8,128)} fusion(f32[4,16,1024]{2,1,0:T(8,128)} %get-tuple-element.1144, s32[]{:T(128)S(6)} %copy.77, f32[16,1024]{1,0:T(8,128)S(1)} %dynamic-slice_bitcast_fusion.2, f32[1024,1024]{0,1:T(8,128)S(1)} %multiply_select_fusion.2), kind=kOutput, calls=%fused_computation.37.clone.1 | convolution fusion | flops 201326592 | bytes 4325380 | tf_op jit(solution)/shard_map/while/body/eval_jaxpr/dot_general | solution.py:97
  134.9 3.8 %fusion.212 = (f32[1024]{0:T(1024)S(1)}, f32[1024,1024]{0,1:T(8,128)S(1)}) fusion(f32[16,1024]{1,0:T(8,128)S(1)} %dynamic-slice_bitcast_fusion.2, f32[4,16,1024]{2,1,0:T(8,128)S(1)} %get-tuple-element.1167, s32[]{:T(128)S(6)} %copy.77), kind=kOutput, calls=%fused_computation.28.clone.1 | convolution fusion | flops 208665600 | bytes 4329476 | tf_op jit(solution)/shard_map/while/body/eval_jaxpr/dot_general | solution.py:76
  149.9 2.1 fusion.217
  152.0 4.2 %fusion.218 = f32[4,16,1024]{2,1,0:T(8,128)} fusion(f32[4,16,1024]{2,1,0:T(8,128)} %get-tuple-element.1144, s32[]{:T(128)S(6)} %copy.77, f32[16,1024]{1,0:T(8,128)S(1)} %dynamic-slice_bitcast_fusion.2, f32[1024,1024]{0,1:T(8,128)S(1)} %multiply_select_fusion.2), kind=kOutput, calls=%fused_computation.37.clone.1 | convolution fusion | flops 201326592 | bytes 4325380 | tf_op jit(solution)/shard_map/while/body/eval_jaxpr/dot_general | solution.py:97
  159.5 3.8 %fusion.212 = (f32[1024]{0:T(1024)S(1)}, f32[1024,1024]{0,1:T(8,128)S(1)}) fusion(f32[16,1024]{1,0:T(8,128)S(1)} %dynamic-slice_bitcast_fusion.2, f32[4,16,1024]{2,1,0:T(8,128)S(1)} %get-tuple-element.1167, s32[]{:T(128)S(6)} %copy.77), kind=kOutput, calls=%fused_computation.28.clone.1 | convolution fusion | flops 208665600 | bytes 4329476 | tf_op jit(solution)/shard_map/while/body/eval_jaxpr/dot_general | solution.py:76
  176.5 4.2 %fusion.218 = f32[4,16,1024]{2,1,0:T(8,128)} fusion(f32[4,16,1024]{2,1,0:T(8,128)} %get-tuple-element.1144, s32[]{:T(128)S(6)} %copy.77, f32[16,1024]{1,0:T(8,128)S(1)} %dynamic-slice_bitcast_fusion.2, f32[1024,1024]{0,1:T(8,128)S(1)} %multiply_select_fusion.2), kind=kOutput, calls=%fused_computation.37.clone.1 | convolution fusion | flops 201326592 | bytes 4325380 | tf_op jit(solution)/shard_map/while/body/eval_jaxpr/dot_general | solution.py:97
  184.0 3.8 %fusion.212 = (f32[1024]{0:T(1024)S(1)}, f32[1024,1024]{0,1:T(8,128)S(1)}) fusion(f32[16,1024]{1,0:T(8,128)S(1)} %dynamic-slice_bitcast_fusion.2, f32[4,16,1024]{2,1,0:T(8,128)S(1)} %get-tuple-element.1167, s32[]{:T(128)S(6)} %copy.77), kind=kOutput, calls=%fused_computation.28.clone.1 | convolution fusion | flops 208665600 | bytes 4329476 | tf_op jit(solution)/shard_map/while/body/eval_jaxpr/dot_general | solution.py:76
  201.0 4.2 %fusion.218 = f32[4,16,1024]{2,1,0:T(8,128)} fusion(f32[4,16,1024]{2,1,0:T(8,128)} %get-tuple-element.1144, s32[]{:T(128)S(6)} %copy.77, f32[16,1024]{1,0:T(8,128)S(1)} %dynamic-slice_bitcast_fusion.2, f32[1024,1024]{0,1:T(8,128)S(1)} %multiply_select_fusion.2), kind=kOutput, calls=%fused_computation.37.clone.1 | convolution fusion | flops 201326592 | bytes 4325380 | tf_op jit(solution)/shard_map/while/body/eval_jaxpr/dot_general | solution.py:97
  207.7 27.9 %all-gather.21.cloned.1.call-done = f32[16,153,128]{2,1,0:T(8,128)} async-done(((f32[4,153,128]{2,1,0:T(8,128)}), f32[16,153,128]{2,1,0:T(8,128)}) %all-gather.21.cloned.1.call-update) | async-done | bytes 1253392 | tf_op jit(solution)/shard_map/all_gather | solution.py:154
  235.6 2.3 fusion.89
  238.0 8.1 %all-gather.10 = f32[4,4,153]{2,1,0:T(4,128)S(1)} all-gather(f32[1,4,153]{2,1,0:T(4,128)S(1)} %bitcast.303), channel_id=8, replica_groups=mesh['seq'=4,'seg'=4,'head'=2] {'seq'}, dimensions={0}, use_global_device_ids=true | all-gather | bytes 12240 | tf_op jit(solution)/shard_map/all_gather | solution.py:155
  246.2 13.7 %all-gather.11 = f32[4,4,153]{2,1,0:T(4,128)S(1)} all-gather(f32[1,4,153]{2,1,0:T(4,128)S(1)} %bitcast.302), channel_id=9, replica_groups=mesh['seq'=4,'seg'=4,'head'=2] {'seg'}, dimensions={0}, use_global_device_ids=true | all-gather | bytes 12240 | tf_op jit(solution)/shard_map/all_gather | solution.py:13
  259.9 10.9 %all-gather.23.cloned.1.call-done = f32[16,153,128]{2,1,0:T(8,128)} async-done(((f32[4,153,128]{2,1,0:T(8,128)}), f32[16,153,128]{2,1,0:T(8,128)}) %all-gather.23.cloned.1.call-update) | async-done | bytes 1253392 | tf_op jit(solution)/shard_map/all_gather | solution.py:13
  272.7 25.7 %while.83 = (s32[]{:T(128)}, f32[4,128,16]{1,2,0:T(8,128)S(1)}, f32[4,128,16]{1,2,0:T(8,128)S(1)}, bf16[4,1024,128]{2,1,0:T(8,128)(2,1)}, bf16[4,16,1024]{2,1,0:...) while((s32[]{:T(128)}, f32[4,128,16]{1,2,0:T(8,128)S(1)}, ...), condition=%wide.region_20.21_spmd.clone, body=%wide.region_19.20_spmd.sunk.clone.sunk | while | flops 156230656 | bytes 5469037 | solution.py:178
  298.4 39.8 %all-reduce = (f32[128,16]{0,1:T(8,128)}, f32[128,16]{0,1:T(8,128)}) all-reduce(f32[128,16]{0,1:T(8,128)S(1)} %reduce_sum.125, f32[128,16]{0,1:T(8,128)S(1)} %reduce_sum.126), channel_id=1, replica_groups=mesh['seq'=4,'seg'=4,'head'=2] {'seq','seg','head'}, use_global_device_ids=true, to_apply=%region_22.23 | all-reduce | flops 4096 | bytes 32768 | tf_op jit(solution)/shard_map/psum | solution.py:182
  (241 shorter events, 127.0 us)
Async XLA Ops:
  7.2 61.0 %all-gather.17.cloned.1.call-start = ((), (), s32[]{:S(2)}) async-start(), calls=%async_computation | async-start | bytes 1638400 | tf_op jit(solution)/shard_map/all_gather | solution.py:154
  35.8 0.7 copy-start.4
  36.6 66.9 %all-gather.19.cloned.1.call-start = ((), (), s32[]{:S(2)}) async-start(), calls=%async_computation.1 | async-start | bytes 1638400 | tf_op jit(solution)/shard_map/all_gather | solution.py:13
  68.1 40.9 %copy-start.2 = (f32[136,16]{1,0:T(8,128)S(1)}, f32[136,16]{1,0:T(8,128)}, u32[]{:S(2)}) copy-start(f32[136,16]{1,0:T(8,128)} %get-tuple-element.1252) | copy-start | bytes 26116
  68.1 40.9 %copy-start.3 = (f32[136,16]{1,0:T(8,128)S(1)}, f32[136,16]{1,0:T(8,128)}, u32[]{:S(2)}) copy-start(f32[136,16]{1,0:T(8,128)} %get-tuple-element.1254) | copy-start | bytes 26116
  68.1 40.9 %copy-start.5 = (f32[136]{0:T(256)S(1)}, f32[136]{0:T(256)}, u32[]{:S(2)}) copy-start(f32[136]{0:T(256)} %get-tuple-element.1271) | copy-start | bytes 1636
  70.5 165.0 %all-gather.21.cloned.1.call-start = ((), (), s32[]{:S(2)}) async-start(), calls=%async_computation.2 | async-start | bytes 1638400 | tf_op jit(solution)/shard_map/all_gather | solution.py:154
  114.3 3.4 copy-start
  119.6 3.9 %copy-start.1 = (f32[1024,1024]{0,1:T(8,128)S(1)}, f32[1024,1024]{0,1:T(8,128)}, u32[]{:S(2)}) copy-start(f32[1024,1024]{0,1:T(8,128)} %copy-done) | copy-start | bytes 12582916 | tf_op jit(solution)/shard_map/while
  123.5 1.9 copy-start.6
  127.4 6.3 %copy-start.7 = (bf16[4,16,1024]{2,1,0:T(8,128)(2,1)}, bf16[4,16,1024]{2,1,0:T(8,128)(2,1)S(1)}, u32[]{:S(2)}) copy-start(bf16[4,16,1024]{2,1,0:T(8,128)(2,1)S(1)} %fusion.217) | copy-start | bytes 393220 | tf_op jit(solution)/shard_map/while
  138.8 3.4 copy-start
  144.1 3.9 %copy-start.1 = (f32[1024,1024]{0,1:T(8,128)S(1)}, f32[1024,1024]{0,1:T(8,128)}, u32[]{:S(2)}) copy-start(f32[1024,1024]{0,1:T(8,128)} %copy-done) | copy-start | bytes 12582916 | tf_op jit(solution)/shard_map/while
  148.0 1.9 copy-start.6
  152.0 6.3 %copy-start.7 = (bf16[4,16,1024]{2,1,0:T(8,128)(2,1)}, bf16[4,16,1024]{2,1,0:T(8,128)(2,1)S(1)}, u32[]{:S(2)}) copy-start(bf16[4,16,1024]{2,1,0:T(8,128)(2,1)S(1)} %fusion.217) | copy-start | bytes 393220 | tf_op jit(solution)/shard_map/while
  163.3 3.4 copy-start
  168.6 3.9 %copy-start.1 = (f32[1024,1024]{0,1:T(8,128)S(1)}, f32[1024,1024]{0,1:T(8,128)}, u32[]{:S(2)}) copy-start(f32[1024,1024]{0,1:T(8,128)} %copy-done) | copy-start | bytes 12582916 | tf_op jit(solution)/shard_map/while
  172.5 1.9 copy-start.6
  176.5 6.3 %copy-start.7 = (bf16[4,16,1024]{2,1,0:T(8,128)(2,1)}, bf16[4,16,1024]{2,1,0:T(8,128)(2,1)S(1)}, u32[]{:S(2)}) copy-start(bf16[4,16,1024]{2,1,0:T(8,128)(2,1)S(1)} %fusion.217) | copy-start | bytes 393220 | tf_op jit(solution)/shard_map/while
  187.8 3.4 copy-start
  193.2 3.9 %copy-start.1 = (f32[1024,1024]{0,1:T(8,128)S(1)}, f32[1024,1024]{0,1:T(8,128)}, u32[]{:S(2)}) copy-start(f32[1024,1024]{0,1:T(8,128)} %copy-done) | copy-start | bytes 12582916 | tf_op jit(solution)/shard_map/while
  197.1 1.9 copy-start.6
  201.0 6.3 %copy-start.7 = (bf16[4,16,1024]{2,1,0:T(8,128)(2,1)}, bf16[4,16,1024]{2,1,0:T(8,128)(2,1)S(1)}, u32[]{:S(2)}) copy-start(bf16[4,16,1024]{2,1,0:T(8,128)(2,1)S(1)} %fusion.217) | copy-start | bytes 393220 | tf_op jit(solution)/shard_map/while
  207.6 63.2 %all-gather.23.cloned.1.call-start = ((), (), s32[]{:S(2)}) async-start(), calls=%async_computation.3 | async-start | bytes 1638400 | tf_op jit(solution)/shard_map/all_gather | solution.py:13
Sparse Core Ops, SparseCore 0:
  36.7 31.3 all-gather.16
  70.7 32.7 all-gather.18
  207.7 27.7 all-gather.20
  238.1 32.7 all-gather.22
where the time goes:
time: 347 us; the launch traced here: 345 us
  matrix products  140 us (40%)
  blocking collectives  83.4 us (24%)
  waiting for transfers between devices  80.6 us (23%)
  between operations  14 us (4%)
  other arithmetic  12.4 us (4%)
  local copies, waits for them, and re-layouts  12.3 us (4%)
    all_gather x2, waiting for transfers between devices, carried(): lax.all_gather(stacked[0], 'seq', axis=0, tiled=True)  59.4 us
    psum x1, blocking collectives, shards(): lax.psum((jnp.sum(grad_q, 0), jnp.sum(grad_k, 0)), ('seq', 'seg', 'head'))  39.8 us
    all_gather x2, blocking collectives, carried_in(): pieces = jax.tree.map(lambda part: lax.all_gather(part, axis), value)  27.4 us
    all_gather x2, waiting for transfers between devices, carried_in(): pieces = jax.tree.map(lambda part: lax.all_gather(part, axis), value)  21.2 us
    dot_general x4, matrix products, head_forward(): g_k = jnp.dot(q_t, g_scores, precision=highest)  16.6 us
    all_gather x2, blocking collectives, carried(): lax.all_gather(stacked[1], 'seq', axis=0, tiled=True)  16.3 us
    dot_general x4, matrix products, head_forward(): lax.dot_general(q_t, k_t, (((0,), (0,)), ((), ())), precision=highest)  15.3 us
    dot_general x8, matrix products, project(): lax.dot_general(weight_b, rows, (((0,), (1,)), ((), ())), preferred_eleme...  9.01 us
  transfers between devices with their start and end apart: 4, of which 4 were waited for; matrix products, arithmetic and copies ran while one was open for 0% of the time, Pallas kernels for 0%

commit v1 on v0

--- a/solution.py
+++ b/solution.py
@@ -6,6 +6,18 @@
 from jax.sharding import PartitionSpec as P
 
 highest = lax.Precision.HIGHEST
+
+
+def doubled_up(x, axis, dim):
+    ways, here = (lax.axis_size(axis), lax.axis_index(axis))
+    grown, reach = (x, 1)
+    while reach < ways:
+        theirs = lax.ppermute(grown, axis, [(d, d ^ reach) for d in range(ways)])
+        mine_first = jnp.concatenate([grown, theirs], axis=dim)
+        theirs_first = jnp.concatenate([theirs, grown], axis=dim)
+        grown = jnp.where(here & reach == 0, mine_first, theirs_first)
+        reach = 2 * reach
+    return grown
 
 
 def carried_in(value, axis, join, neutral, backward):
@@ -150,10 +162,7 @@
         lax.axis_index("seq"),
         backward,
         (zeros, zeros),
-        (
-            lax.all_gather(stacked[0], "seq", axis=0, tiled=True),
-            lax.all_gather(stacked[1], "seq", axis=0, tiled=True),
-        ),
+        (doubled_up(stacked[0], "seq", 0), lax.all_gather(stacked[1], "seq", axis=0, tiled=True)),
     )
     outer = carried_in(totals, "seg", add_trees, zeros, backward)
     return add_trees(inner, outer)

time: 347 us -> 362 us (1.043)
  local copies, waits for them, and re-layouts: 12.3 us -> 48.9 us
  waiting for transfers between devices: 80.6 us -> 63.4 us
  matrix products: 140 us -> 129 us
  starting transfers between devices: 0.16 us -> 7.93 us
    all_gather x2 -> x0, waiting for transfers between devices: 59.4 us -> none  [carried(): lax.all_gather(stacked[0], 'seq', axis=0, tiled=True)]
    ppermute x0 -> x4, waiting for transfers between devices: none -> 40.8 us  [doubled_up(): theirs = lax.ppermute(grown, axis, [(d, d ^ reach) for d in range(ways)])]
    dynamic_update_slice x8 -> x24, local copies, waits for them, and re-layouts: 0.35 us -> 31 us  [shards(): lax.map(lambda xs: head_state(xs[0], xs[1], xs[2], wq_b, wk_b, tables), (...]
    ppermute x0 -> x4, starting transfers between devices: none -> 7.85 us  [doubled_up(): theirs = lax.ppermute(grown, axis, [(d, d ^ reach) for d in range(ways)])]
    dot_general x4, matrix products: 8.28 us -> 2.89 us  [head_forward(): lax.dot_general(s_prev, g_numer, (((1,), (1,)), ((), ())), precision=high...]
    dynamic_slice x8 -> x16, local copies, waits for them, and re-layouts: 0.06 us -> 4.59 us  [shards(): lax.map(lambda xs: head_forward(xs[0], xs[1], xs[2], xs[3], xs[4], xs[5],...]
  transfers between devices with their start and end apart: 4 -> 6, of which waited for: 4 -> 6; matrix products, arithmetic and copies ran while one was open for 0% -> 0% of each run, Pallas kernels for 0% -> 0%
where the time goes in v1:
time: 362 us; the launch traced here: 360 us
  matrix products  129 us (36%)
  blocking collectives  84 us (23%)
  waiting for transfers between devices  63.4 us (18%)
  local copies, waits for them, and re-layouts  48.9 us (14%)
  between operations  14.2 us (4%)
  other arithmetic  10.9 us (3%)
  starting transfers between devices  7.93 us (2%)
    ppermute x4, waiting for transfers between devices, doubled_up(): theirs = lax.ppermute(grown, axis, [(d, d ^ reach) for d in range(ways)])  40.8 us
    psum x1, blocking collectives, shards(): lax.psum((jnp.sum(grad_q, 0), jnp.sum(grad_k, 0)), ('seq', 'seg', 'head'))  39.8 us
    dynamic_update_slice x24, local copies, waits for them, and re-layouts, shards(): lax.map(lambda xs: head_state(xs[0], xs[1], xs[2], wq_b, wk_b, tables), (...  31 us
    all_gather x2, blocking collectives, carried_in(): pieces = jax.tree.map(lambda part: lax.all_gather(part, axis), value)  27.7 us
    all_gather x2, waiting for transfers between devices, carried_in(): pieces = jax.tree.map(lambda part: lax.all_gather(part, axis), value)  22.6 us
    dot_general x4, matrix products, head_forward(): g_k = jnp.dot(q_t, g_scores, precision=highest)  16.6 us
    all_gather x2, blocking collectives, carried(): lax.all_gather(stacked[1], 'seq', axis=0, tiled=True)  16.6 us
    dot_general x4, matrix products, head_forward(): lax.dot_general(q_t, k_t, (((0,), (0,)), ((), ())), precision=highest)  15.3 us
  transfers between devices with their start and end apart: 6, of which 6 were waited for; matrix products, arithmetic and copies ran while one was open for 0% of the time, Pallas kernels for 0%

profile of v1, /device:TPU:0, one launch (start us, length us, event | category | flops | bytes accessed | tf_op | source)
XLA Modules:
  0.0 359.7 jit_solution(15789962234656111245)
XLA Ops:
  8.7 38.0 %while.81 = (s32[]{:T(128)}, f32[4,16,1024]{2,1,0:T(8,128)S(1)}, f32[4,16,1024]{2,1,0:T(8,128)S(1)}, f32[4,153,128]{2,0,1:T(4,128)S(1)}, f32[4,153]{1,0:T(4,128)...) while((s32[]{:T(128)}, f32[4,16,1024]{2,1,0:T(8,128)S(1)}, ...), condition=%wide.region_2.3_spmd.clone, body=%wide.region_0.2_spmd.sunk.clone.sunk | while | flops 103662440 | bytes 4454193 | solution.py:175
  49.7 7.4 %collective-permute-done = f32[1,4,153,128]{3,1,2,0:T(4,128)S(1)} collective-permute-done((f32[1,4,153,128]{3,1,2,0:T(4,128)S(1)}, f32[1,4,153,128]{3,1,2,0:T(4,128)S(1)}, u32[]{:S(2)}, u32[]{:S(2)}) %collective-permute-start) | collective-permute-done | bytes 313376 | tf_op jit(solution)/shard_map/ppermute | solution.py:15
  59.1 13.5 %collective-permute-done.1 = f32[2,4,153,128]{3,1,2,0:T(4,128)S(1)} collective-permute-done((f32[2,4,153,128]{3,1,2,0:T(4,128)S(1)}, f32[2,4,153,128]{3,1,2,0:T(4,128)S(1)}, u32[]{:S(2)}, u32[]{:S(2)}) %collective-permute-start.1) | collective-permute-done | bytes 626720 | tf_op jit(solution)/shard_map/ppermute | solution.py:15
  74.2 8.2 %all-gather.6 = f32[4,4,153]{2,1,0:T(4,128)S(1)} all-gather(f32[1,4,153]{2,1,0:T(4,128)S(1)} %bitcast.301), channel_id=3, replica_groups=mesh['seq'=4,'seg'=4,'head'=2] {'seq'}, dimensions={0}, use_global_device_ids=true | all-gather | bytes 12240 | tf_op jit(solution)/shard_map/all_gather | solution.py:165
  82.5 13.7 %all-gather.7 = f32[4,4,153]{2,1,0:T(4,128)S(1)} all-gather(f32[1,4,153]{2,1,0:T(4,128)S(1)} %bitcast.298), channel_id=4, replica_groups=mesh['seq'=4,'seg'=4,'head'=2] {'seg'}, dimensions={0}, use_global_device_ids=true | all-gather | bytes 12240 | tf_op jit(solution)/shard_map/all_gather | solution.py:25
  96.9 11.4 %all-gather.13.cloned.1.call-done = f32[16,153,128]{2,1,0:T(8,128)} async-done(((f32[4,153,128]{2,1,0:T(8,128)}), f32[16,153,128]{2,1,0:T(8,128)}) %all-gather.13.cloned.1.call-update) | async-done | bytes 1253392 | tf_op jit(solution)/shard_map/all_gather | solution.py:25
  114.7 110.8 %while.82 = (s32[]{:T(128)}, bf16[4,1024,128]{2,1,0:T(8,128)(2,1)}, bf16[4,16,1024]{2,1,0:T(8,128)(2,1)}, f32[4,16,1024]{2,1,0:T(8,128)}, f32[4,153,128]{2,0,1:T...) while((s32[]{:T(128)}, bf16[4,1024,128]{2,1,0:T(8,128)(2,1)}, ...), condition=%wide.region_12.13_spmd.clone, body=%wide.region_9.12_spmd.sunk.clone.sunk | while | flops 1998507008 | bytes 76341792 | solution.py:182
  116.1 3.8 %fusion.199 = (f32[1024]{0:T(1024)S(1)}, f32[1024,1024]{0,1:T(8,128)S(1)}) fusion(f32[16,1024]{1,0:T(8,128)S(1)} %dynamic-slice_bitcast_fusion.2, f32[4,16,1024]{2,1,0:T(8,128)S(1)} %get-tuple-element.1190, s32[]{:T(128)S(6)} %copy.117), kind=kOutput, calls=%fused_computation.27.clone.1 | convolution fusion | flops 208665600 | bytes 4329476 | tf_op jit(solution)/shard_map/while/body/eval_jaxpr/dot_general | solution.py:88
  131.9 4.2 %fusion.205 = f32[4,16,1024]{2,1,0:T(8,128)} fusion(f32[4,16,1024]{2,1,0:T(8,128)} %get-tuple-element.1167, s32[]{:T(128)S(6)} %copy.117, f32[16,1024]{1,0:T(8,128)S(1)} %dynamic-slice_bitcast_fusion.2, f32[1024,1024]{0,1:T(8,128)S(1)} %multiply_select_fusion.2), kind=kOutput, calls=%fused_computation.35.clone.1 | convolution fusion | flops 201326592 | bytes 4325380 | tf_op jit(solution)/shard_map/while/body/eval_jaxpr/dot_general | solution.py:109
  136.9 3.6 %dynamic_update_slice.85 = f32[4,153,128]{2,0,1:T(4,128)} dynamic-update-slice(f32[4,153,128]{2,0,1:T(4,128)} %get-tuple-element.1168, f32[1,153,128]{2,0,1:T(1,128)S(1)} %copy.74, s32[]{:T(128)S(6)} %copy.117, s32[]{:T(128)} %constant.132.clone.1..sunk.1, s32[]{:T(128)} %constant.132.clone.1..sunk.1) | dynamic-update-slice | bytes 156676 | tf_op jit(solution)/shard_map/while/body/jit(dynamic_update_index_in_dim)/dynamic_update_slice | solution.py:175
  143.7 3.8 %fusion.199 = (f32[1024]{0:T(1024)S(1)}, f32[1024,1024]{0,1:T(8,128)S(1)}) fusion(f32[16,1024]{1,0:T(8,128)S(1)} %dynamic-slice_bitcast_fusion.2, f32[4,16,1024]{2,1,0:T(8,128)S(1)} %get-tuple-element.1190, s32[]{:T(128)S(6)} %copy.117), kind=kOutput, calls=%fused_computation.27.clone.1 | convolution fusion | flops 208665600 | bytes 4329476 | tf_op jit(solution)/shard_map/while/body/eval_jaxpr/dot_general | solution.py:88
  159.6 4.2 %fusion.205 = f32[4,16,1024]{2,1,0:T(8,128)} fusion(f32[4,16,1024]{2,1,0:T(8,128)} %get-tuple-element.1167, s32[]{:T(128)S(6)} %copy.117, f32[16,1024]{1,0:T(8,128)S(1)} %dynamic-slice_bitcast_fusion.2, f32[1024,1024]{0,1:T(8,128)S(1)} %multiply_select_fusion.2), kind=kOutput, calls=%fused_computation.35.clone.1 | convolution fusion | flops 201326592 | bytes 4325380 | tf_op jit(solution)/shard_map/while/body/eval_jaxpr/dot_general | solution.py:109
  171.4 3.8 %fusion.199 = (f32[1024]{0:T(1024)S(1)}, f32[1024,1024]{0,1:T(8,128)S(1)}) fusion(f32[16,1024]{1,0:T(8,128)S(1)} %dynamic-slice_bitcast_fusion.2, f32[4,16,1024]{2,1,0:T(8,128)S(1)} %get-tuple-element.1190, s32[]{:T(128)S(6)} %copy.117), kind=kOutput, calls=%fused_computation.27.clone.1 | convolution fusion | flops 208665600 | bytes 4329476 | tf_op jit(solution)/shard_map/while/body/eval_jaxpr/dot_general | solution.py:88
  187.2 4.2 %fusion.205 = f32[4,16,1024]{2,1,0:T(8,128)} fusion(f32[4,16,1024]{2,1,0:T(8,128)} %get-tuple-element.1167, s32[]{:T(128)S(6)} %copy.117, f32[16,1024]{1,0:T(8,128)S(1)} %dynamic-slice_bitcast_fusion.2, f32[1024,1024]{0,1:T(8,128)S(1)} %multiply_select_fusion.2), kind=kOutput, calls=%fused_computation.35.clone.1 | convolution fusion | flops 201326592 | bytes 4325380 | tf_op jit(solution)/shard_map/while/body/eval_jaxpr/dot_general | solution.py:109
  192.3 3.6 %dynamic_update_slice.85 = f32[4,153,128]{2,0,1:T(4,128)} dynamic-update-slice(f32[4,153,128]{2,0,1:T(4,128)} %get-tuple-element.1168, f32[1,153,128]{2,0,1:T(1,128)S(1)} %copy.74, s32[]{:T(128)S(6)} %copy.117, s32[]{:T(128)} %constant.132.clone.1..sunk.1, s32[]{:T(128)} %constant.132.clone.1..sunk.1) | dynamic-update-slice | bytes 156676 | tf_op jit(solution)/shard_map/while/body/jit(dynamic_update_index_in_dim)/dynamic_update_slice | solution.py:175
  199.0 3.8 %fusion.199 = (f32[1024]{0:T(1024)S(1)}, f32[1024,1024]{0,1:T(8,128)S(1)}) fusion(f32[16,1024]{1,0:T(8,128)S(1)} %dynamic-slice_bitcast_fusion.2, f32[4,16,1024]{2,1,0:T(8,128)S(1)} %get-tuple-element.1190, s32[]{:T(128)S(6)} %copy.117), kind=kOutput, calls=%fused_computation.27.clone.1 | convolution fusion | flops 208665600 | bytes 4329476 | tf_op jit(solution)/shard_map/while/body/eval_jaxpr/dot_general | solution.py:88
  214.9 4.2 %fusion.205 = f32[4,16,1024]{2,1,0:T(8,128)} fusion(f32[4,16,1024]{2,1,0:T(8,128)} %get-tuple-element.1167, s32[]{:T(128)S(6)} %copy.117, f32[16,1024]{1,0:T(8,128)S(1)} %dynamic-slice_bitcast_fusion.2, f32[1024,1024]{0,1:T(8,128)S(1)} %multiply_select_fusion.2), kind=kOutput, calls=%fused_computation.35.clone.1 | convolution fusion | flops 201326592 | bytes 4325380 | tf_op jit(solution)/shard_map/while/body/eval_jaxpr/dot_general | solution.py:109
  227.0 7.1 %collective-permute-done.2 = f32[1,4,153,128]{3,1,2,0:T(4,128)S(1)} collective-permute-done((f32[1,4,153,128]{3,1,2,0:T(4,128)}, f32[1,4,153,128]{3,1,2,0:T(4,128)S(1)}, u32[]{:S(2)}, u32[]{:S(2)}) %collective-permute-start.2) | collective-permute-done | bytes 313376 | tf_op jit(solution)/shard_map/ppermute | solution.py:15
  237.0 12.7 %collective-permute-done.3 = f32[2,4,153,128]{3,1,2,0:T(4,128)S(1)} collective-permute-done((f32[2,4,153,128]{3,1,2,0:T(4,128)S(1)}, f32[2,4,153,128]{3,1,2,0:T(4,128)S(1)}, u32[]{:S(2)}, u32[]{:S(2)}) %collective-permute-start.3) | collective-permute-done | bytes 626720 | tf_op jit(solution)/shard_map/ppermute | solution.py:15
  251.2 8.4 %all-gather.8 = f32[4,4,153]{2,1,0:T(4,128)S(1)} all-gather(f32[1,4,153]{2,1,0:T(4,128)} %bitcast.300), channel_id=6, replica_groups=mesh['seq'=4,'seg'=4,'head'=2] {'seq'}, dimensions={0}, use_global_device_ids=true | all-gather | bytes 12240 | tf_op jit(solution)/shard_map/all_gather | solution.py:165
  259.7 14.0 %all-gather.9 = f32[4,4,153]{2,1,0:T(4,128)S(1)} all-gather(f32[1,4,153]{2,1,0:T(4,128)S(1)} %bitcast.299), channel_id=7, replica_groups=mesh['seq'=4,'seg'=4,'head'=2] {'seg'}, dimensions={0}, use_global_device_ids=true | all-gather | bytes 12240 | tf_op jit(solution)/shard_map/all_gather | solution.py:25
  273.7 11.2 %all-gather.15.cloned.1.call-done = f32[16,153,128]{2,1,0:T(8,128)} async-done(((f32[4,153,128]{2,1,0:T(8,128)}), f32[16,153,128]{2,1,0:T(8,128)}) %all-gather.15.cloned.1.call-update) | async-done | bytes 1253392 | tf_op jit(solution)/shard_map/all_gather | solution.py:25
  287.0 26.0 %while.83 = (s32[]{:T(128)}, f32[4,128,16]{1,2,0:T(8,128)S(1)}, f32[4,128,16]{1,2,0:T(8,128)S(1)}, bf16[4,1024,128]{2,1,0:T(8,128)(2,1)}, bf16[4,16,1024]{2,1,0:...) while((s32[]{:T(128)}, f32[4,128,16]{1,2,0:T(8,128)S(1)}, ...), condition=%wide.region_20.21_spmd.clone, body=%wide.region_19.20_spmd.sunk.clone.sunk | while | flops 156230656 | bytes 5544153 | solution.py:187
  313.1 39.8 %all-reduce = (f32[128,16]{0,1:T(8,128)}, f32[128,16]{0,1:T(8,128)}) all-reduce(f32[128,16]{0,1:T(8,128)S(1)} %reduce_sum.125, f32[128,16]{0,1:T(8,128)S(1)} %reduce_sum.126), channel_id=1, replica_groups=mesh['seq'=4,'seg'=4,'head'=2] {'seq','seg','head'}, use_global_device_ids=true, to_apply=%region_22.23 | all-reduce | flops 4096 | bytes 32768 | tf_op jit(solution)/shard_map/psum | solution.py:191
  (269 shorter events, 161.3 us)
Async XLA Ops:
  7.2 101.1 %all-gather.13.cloned.1.call-start = ((), (), s32[]{:S(2)}) async-start(), calls=%async_computation | async-start | bytes 1638400 | tf_op jit(solution)/shard_map/all_gather | solution.py:25
  46.7 10.4 %collective-permute-start = (f32[1,4,153,128]{3,1,2,0:T(4,128)S(1)}, f32[1,4,153,128]{3,1,2,0:T(4,128)S(1)}, u32[]{:S(2)}, u32[]{:S(2)}) collective-permute-start(f32[1,4,153,128]{3,1,2,0:T(4,128)S(1)} %bitcast.291), channel_id=1, source_target_pairs={{0,8},{8,0},{16,24},{24,16},{1,9},{9,1},{17,25},{25,17},{2,10},{10... | collective-permute-start | bytes 940040 | tf_op jit(solution)/shard_map/ppermute | solution.py:15
  57.3 15.4 %collective-permute-start.1 = (f32[2,4,153,128]{3,1,2,0:T(4,128)S(1)}, f32[2,4,153,128]{3,1,2,0:T(4,128)S(1)}, u32[]{:S(2)}, u32[]{:S(2)}) collective-permute-start(f32[2,4,153,128]{3,1,2,0:T(4,128)S(1)} %maximum_select_fusion.2), channel_id=1, source_target_pairs={{0,16},{8,24},{16,0},{24,8},{1,17},{9,25},{17,1},{25,9},{2,18},{10... | collective-permute-start | bytes 1880072 | tf_op jit(solution)/shard_map/ppermute | solution.py:15
  73.3 41.4 %copy-start.2 = (f32[136,16]{1,0:T(8,128)S(1)}, f32[136,16]{1,0:T(8,128)}, u32[]{:S(2)}) copy-start(f32[136,16]{1,0:T(8,128)} %get-tuple-element.1273) | copy-start | bytes 26116
  73.3 41.4 %copy-start.3 = (f32[136,16]{1,0:T(8,128)S(1)}, f32[136,16]{1,0:T(8,128)}, u32[]{:S(2)}) copy-start(f32[136,16]{1,0:T(8,128)} %get-tuple-element.1275) | copy-start | bytes 26116
  73.4 41.4 %copy-start.4 = (f32[136]{0:T(256)S(1)}, f32[136]{0:T(256)}, u32[]{:S(2)}) copy-start(f32[136]{0:T(256)} %get-tuple-element.1290) | copy-start | bytes 1636
  74.2 210.7 %all-gather.15.cloned.1.call-start = ((), (), s32[]{:S(2)}) async-start(), calls=%async_computation.1 | async-start | bytes 1638400 | tf_op jit(solution)/shard_map/all_gather | solution.py:25
  119.9 3.4 copy-start
  125.4 2.6 copy-start.1
  127.9 1.9 copy-start.5
  131.9 10.7 %copy-start.6 = (bf16[4,16,1024]{2,1,0:T(8,128)(2,1)}, bf16[4,16,1024]{2,1,0:T(8,128)(2,1)S(1)}, u32[]{:S(2)}) copy-start(bf16[4,16,1024]{2,1,0:T(8,128)(2,1)S(1)} %fusion.204) | copy-start | bytes 393220 | tf_op jit(solution)/shard_map/while
  147.6 3.4 copy-start
  153.0 2.6 copy-start.1
  155.6 1.9 copy-start.5
  159.6 10.7 %copy-start.6 = (bf16[4,16,1024]{2,1,0:T(8,128)(2,1)}, bf16[4,16,1024]{2,1,0:T(8,128)(2,1)S(1)}, u32[]{:S(2)}) copy-start(bf16[4,16,1024]{2,1,0:T(8,128)(2,1)S(1)} %fusion.204) | copy-start | bytes 393220 | tf_op jit(solution)/shard_map/while
  175.2 3.4 copy-start
  180.7 2.6 copy-start.1
  183.3 1.9 copy-start.5
  187.2 10.7 %copy-start.6 = (bf16[4,16,1024]{2,1,0:T(8,128)(2,1)}, bf16[4,16,1024]{2,1,0:T(8,128)(2,1)S(1)}, u32[]{:S(2)}) copy-start(bf16[4,16,1024]{2,1,0:T(8,128)(2,1)S(1)} %fusion.204) | copy-start | bytes 393220 | tf_op jit(solution)/shard_map/while
  202.9 3.4 copy-start
  208.4 2.6 copy-start.1
  214.9 10.7 %copy-start.6 = (bf16[4,16,1024]{2,1,0:T(8,128)(2,1)}, bf16[4,16,1024]{2,1,0:T(8,128)(2,1)S(1)}, u32[]{:S(2)}) copy-start(bf16[4,16,1024]{2,1,0:T(8,128)(2,1)S(1)} %fusion.204) | copy-start | bytes 393220 | tf_op jit(solution)/shard_map/while
  225.6 8.6 %collective-permute-start.2 = (f32[1,4,153,128]{3,1,2,0:T(4,128)}, f32[1,4,153,128]{3,1,2,0:T(4,128)S(1)}, u32[]{:S(2)}, u32[]{:S(2)}) collective-permute-start(f32[1,4,153,128]{3,1,2,0:T(4,128)} %bitcast.289), channel_id=1, source_target_pairs={{0,8},{8,0},{16,24},{24,16},{1,9},{9,1},{17,25},{25,17},{2,10},{10... | collective-permute-start | bytes 940040 | tf_op jit(solution)/shard_map/ppermute | solution.py:15
  235.4 14.3 %collective-permute-start.3 = (f32[2,4,153,128]{3,1,2,0:T(4,128)S(1)}, f32[2,4,153,128]{3,1,2,0:T(4,128)S(1)}, u32[]{:S(2)}, u32[]{:S(2)}) collective-permute-start(f32[2,4,153,128]{3,1,2,0:T(4,128)S(1)} %maximum_select_fusion.3), channel_id=1, source_target_pairs={{0,16},{8,24},{16,0},{24,8},{1,17},{9,25},{17,1},{25,9},{2,18},{10... | collective-permute-start | bytes 1880072 | tf_op jit(solution)/shard_map/ppermute | solution.py:15
  (1 other events, 1.9 us)
Sparse Core Ops, SparseCore 0:
  74.3 33.9 all-gather.12
  251.3 33.5 all-gather.14
